TPU v7x, 32 devices: a whole 2x2x4 slice. The times are simulated.
32 devices in a mesh: row: 4 (over y, x), col: 8 (over z, core).
Axes of the slice: x: 2, y: 2, z: 4, core: 2. Of those that a mesh axis runs over, the one named last changes fastest.
Arguments:
- pair_act: float32 [768, 768, 128], P('row', 'col'), may hold values from -6 to 6
- grad_out: float32 [768, 768, 128], P('row', 'col'), may hold values from -6 to 6
- residue_mask: int32 [768], replicated, may hold values from 0 to 1, as said below
- norm_gains: float32 [2, 128], replicated, may hold values from 0.25 to 1.75
- weights: float32 [6, 128, 128], replicated, may hold values from -0.5 to 0.5
Outputs:
- grad_pair: float32 [768, 768, 128], P('row', 'col')
- grad_weights: float32 [6, 128, 128], replicated
- grad_gains: float32 [2, 128], replicated
Inputs may be any that keep to these rules, and one draw needn't show every extreme that they name: `residue_mask`: the residues form four stretches of 192; in each stretch the valid residues are a prefix of at least 96 and fewer than 192 residues.
All inputs are finite; a program needn't handle non-finite values.
Results may differ from a plain program's by a relative error of at most 0.00009.
Values sent between devices are 32-bit elements; how exact they have to be, the bound alone decides.
No kernel may reach another device: no remote copies, remote signals or barrier semaphores. Data moves between devices by JAX's collectives and lax.ppermute only.
A program may use at most 320 MiB of HBM per device.

v0:
```python
import jax
import jax.numpy as jnp
from jax import lax
from jax.sharding import PartitionSpec as P

epsilon = 1e-05
highest = lax.Precision.HIGHEST


def norm_parts(operand):
    average = jnp.mean(operand, axis=-1, keepdims=True)
    centered = operand - average
    inv_std = lax.rsqrt(jnp.mean(centered * centered, axis=-1, keepdims=True) + epsilon)
    return (centered * inv_std, inv_std)


def norm_back(grad_hat, normed, inv_std):
    first_mean = jnp.mean(grad_hat, axis=-1, keepdims=True)
    second_mean = jnp.mean(grad_hat * normed, axis=-1, keepdims=True)
    return inv_std * (grad_hat - first_mean - normed * second_mean)


def project(operand, weight):
    return jnp.einsum("ijc,cd->ijd", operand, weight, precision=highest)


def sigmoid(operand):
    return 1.0 / (1.0 + jnp.exp(-operand))


def channel_major(tiles):
    return jnp.transpose(tiles, (0, 3, 1, 2))


def arrange_direct(arrived, tile_rows, tile_cols):
    row_count = lax.axis_size("row")
    col_count = lax.axis_size("col")
    stack_count = arrived.shape[0]
    local_chans = arrived.shape[1]
    shaped = arrived.reshape(stack_count, local_chans, row_count, col_count, tile_rows, tile_cols)
    shaped = jnp.transpose(shaped, (0, 1, 2, 4, 3, 5))
    return shaped.reshape(stack_count, local_chans, row_count * tile_rows, col_count * tile_cols)


def split_direct(chan_stack, tile_rows, tile_cols):
    row_count = lax.axis_size("row")
    col_count = lax.axis_size("col")
    stack_count = chan_stack.shape[0]
    local_chans = chan_stack.shape[1]
    shaped = chan_stack.reshape(
        stack_count, local_chans, row_count, tile_rows, col_count, tile_cols
    )
    shaped = jnp.transpose(shaped, (0, 2, 4, 1, 3, 5))
    return shaped.reshape(stack_count, row_count * col_count, local_chans, tile_rows, tile_cols)


def back_positions(arrived, tile_rows, tile_cols):
    stack_count = arrived.shape[0]
    return jnp.transpose(arrived.reshape(stack_count, -1, tile_rows, tile_cols), (0, 2, 3, 1))


def acts_to_channels(stacked, tile_rows, tile_cols):
    arrived = lax.all_to_all(stacked, ("row", "col"), split_axis=1, concat_axis=2, tiled=True)
    result = arrange_direct(arrived, tile_rows, tile_cols)
    return result


def dtri_to_channels(stacked, tile_rows, tile_cols):
    arrived = lax.all_to_all(stacked, ("row", "col"), split_axis=1, concat_axis=2, tiled=True)
    result = arrange_direct(arrived, tile_rows, tile_cols)
    return result


def tri_to_positions(chan_stack, tile_rows, tile_cols):
    arrived = lax.all_to_all(
        split_direct(chan_stack, tile_rows, tile_cols),
        ("row", "col"),
        split_axis=1,
        concat_axis=1,
        tiled=True,
    )
    return back_positions(arrived, tile_rows, tile_cols)


def grads_to_positions(chan_stack, tile_rows, tile_cols):
    arrived = lax.all_to_all(
        split_direct(chan_stack, tile_rows, tile_cols),
        ("row", "col"),
        split_axis=1,
        concat_axis=1,
        tiled=True,
    )
    return back_positions(arrived, tile_rows, tile_cols)


def on_device(pair_act, grad_out, residue_mask, norm_gains, weights):
    tile_rows, tile_cols, channels = pair_act.shape
    residues = residue_mask.shape[0]
    row_mask = lax.dynamic_slice_in_dim(residue_mask, lax.axis_index("row") * tile_rows, tile_rows)
    col_mask = lax.dynamic_slice_in_dim(residue_mask, lax.axis_index("col") * tile_cols, tile_cols)
    pair_mask = (row_mask[:, None] * col_mask[None, :]).astype(jnp.float32)[:, :, None]
    pair_hat, inv_std = norm_parts(pair_act)
    normed = pair_hat * norm_gains[0]
    lin_a = project(normed, weights[0])
    sig_a = sigmoid(project(normed, weights[1]))
    lin_b = project(normed, weights[2])
    sig_b = sigmoid(project(normed, weights[3]))
    act_stack = jnp.stack([pair_mask * sig_a * lin_a, pair_mask * sig_b * lin_b])
    chan_acts = acts_to_channels(channel_major(act_stack), tile_rows, tile_cols)
    chan_tri = jnp.einsum("lik,ljk->lij", chan_acts[0], chan_acts[1], precision=highest)
    triangle = tri_to_positions(chan_tri[None], tile_rows, tile_cols)[0]
    tri_hat, tri_inv = norm_parts(triangle)
    tri_norm = tri_hat * norm_gains[1]
    lin_o = project(tri_norm, weights[5])
    sig_g = sigmoid(project(normed, weights[4]))
    d_out = grad_out * sig_g
    d_gate = grad_out * lin_o * sig_g * (1.0 - sig_g)
    d_norm = project(d_out, weights[5].T)
    d_tri = norm_back(d_norm * norm_gains[1], tri_hat, tri_inv)
    chan_dtri = dtri_to_channels(channel_major(d_tri[None]), tile_rows, tile_cols)[0]
    chan_da = jnp.einsum("lij,ljk->lik", chan_dtri, chan_acts[1], precision=highest)
    chan_db = jnp.einsum("lij,lik->ljk", chan_dtri, chan_acts[0], precision=highest)
    d_acts = grads_to_positions(jnp.stack([chan_da, chan_db]), tile_rows, tile_cols)
    d_lin_a = d_acts[0] * pair_mask * sig_a
    d_sig_a = d_acts[0] * pair_mask * lin_a * sig_a * (1.0 - sig_a)
    d_lin_b = d_acts[1] * pair_mask * sig_b
    d_sig_b = d_acts[1] * pair_mask * lin_b * sig_b * (1.0 - sig_b)
    grads_cat = jnp.concatenate([d_lin_a, d_sig_a, d_lin_b, d_sig_b, d_gate], axis=-1).reshape(
        -1, 5 * channels
    )
    weights_turned = jnp.transpose(weights[:5], (0, 2, 1)).reshape(5 * channels, channels)
    d_normed = jnp.dot(grads_cat, weights_turned, precision=highest).reshape(
        tile_rows, tile_cols, channels
    )
    flat_normed = normed.reshape(-1, channels)
    weight_part = jnp.einsum("pc,pd->cd", flat_normed, grads_cat, precision=highest)
    weight_part = jnp.transpose(weight_part.reshape(channels, 5, channels), (1, 0, 2)).reshape(
        5 * channels, channels
    )
    out_part = jnp.einsum(
        "pc,pd->cd", tri_norm.reshape(-1, channels), d_out.reshape(-1, channels), precision=highest
    )
    gain_one = jnp.sum(d_normed * pair_hat, axis=(0, 1))
    gain_two = jnp.sum(d_norm * tri_hat, axis=(0, 1))
    grad_pair = norm_back(d_normed * norm_gains[0], pair_hat, inv_std)
    combined = jnp.concatenate([weight_part, out_part, gain_one[None], gain_two[None]], axis=0)
    column_total = lax.psum(combined, "col")
    total = lax.psum(column_total, "row")
    scaled = total / residues
    grad_weights = scaled[: 6 * channels].reshape(6, channels, channels)
    grad_gains = scaled[6 * channels :]
    return (grad_pair, grad_weights, grad_gains)


def solution(mesh):
    return jax.shard_map(
        on_device,
        mesh=mesh,
        in_specs=(P("row", "col", None), P("row", "col", None), P(), P(), P()),
        out_specs=(P("row", "col", None), P(), P()),
        check_vma=False,
    )
```

profile of v0, /device:TPU:0, one launch (start us, length us, event | category | flops | bytes accessed | tf_op | source)
XLA Modules:
  0.0 2525.7 jit_solution(4730244408354005469)
XLA Ops:
  14.2 8.4 multiply_reduce_fusion.5
  23.8 7.0 fusion.10
  30.8 10.0 add_divide_fusion.1
  40.8 9.9 add_divide_fusion.2
  50.7 10.0 fusion.31
  60.7 10.0 fusion.34
  72.3 17.6 multiply_bitcast_fusion.2
  89.9 10.8 maximum_bitcast_fusion.1
  100.7 22.2 copy.27
  122.9 551.8 %all_to_all.40 = f32[2,128,192,96]{3,2,0,1:T(8,128)S(1)} all-to-all(f32[2,128,192,96]{3,2,0,1:T(8,128)} %copy.27), channel_id=1, replica_groups=mesh['row'=4,'col'=8] {'row','col'}, dimensions={1} | all-to-all | bytes 37748736 | tf_op jit(solution)/shard_map/all_to_all | solution.py:63
  674.7 28.3 %copy.48 = f32[2,4,4,8,192,96]{5,3,4,2,1,0:T(8,128)} copy(f32[2,4,4,8,192,96]{5,4,0,1,3,2:T(8,128)S(1)} %bitcast.173) | data formatting | bytes 37748736 | tf_op jit(solution)/shard_map/reshape | solution.py:40
  703.0 18.3 fusion.44
  721.3 13.4 squeeze.42
  734.7 13.4 squeeze.43
  748.1 27.5 %fusion.45 = f32[4,768,768]{2,1,0:T(8,128)} fusion(f32[4,768,768]{2,1,0:T(8,128)} %squeeze.42, f32[4,768,768]{2,1,0:T(8,128)} %squeeze.43), kind=kOutput, calls=%fused_computation.81 | convolution fusion | flops 21743271936 | bytes 28311552 | tf_op jit(solution)/shard_map/lik,ljk->lij/dot_general | solution.py:110
  775.6 13.7 reshape_broadcast_in_dim.3
  789.3 11.4 copy.30
  804.9 12.0 add_divide_fusion
  816.9 262.6 %all-to-all-done.1 = f32[1,32,4,192,96]{4,3,2,0,1:T(8,128)} async-done(((f32[1,32,4,192,96]{4,3,2,0,1:T(8,128)}), f32[1,32,4,192,96]{4,3,2,0,1:T(8,128)}, u32[]{:S(2)}, u32[]{:S(2)}) %all-to-all-start.1) | async-done | bytes 9437216 | tf_op jit(solution)/shard_map/all_to_all | solution.py:75
  1079.6 11.7 copy.32
  1091.3 7.1 bitcast_reduce_fusion
  1104.8 18.9 multiply_reduce_fusion
  1123.7 12.3 multiply_bitcast_fusion
  1136.0 11.5 copy.33
  1147.5 278.6 %all_to_all.41 = f32[1,128,192,96]{3,2,0,1:T(8,128)} all-to-all(f32[1,128,192,96]{3,2,0,1:T(8,128)} %copy.33), channel_id=1, replica_groups=mesh['row'=4,'col'=8] {'row','col'}, dimensions={1} | all-to-all | bytes 18874368 | tf_op jit(solution)/shard_map/all_to_all | solution.py:69
  1426.1 18.9 copy.49
  1444.9 13.4 squeeze_reshape.3
  1458.3 27.3 %fusion.46 = f32[4,768,768]{2,1,0:T(8,128)} fusion(f32[4,768,768]{2,1,0:T(8,128)} %squeeze_reshape.3, f32[4,768,768]{2,1,0:T(8,128)} %squeeze.43), kind=kOutput, calls=%fused_computation.82 | convolution fusion | flops 21743271936 | bytes 28311552 | tf_op jit(solution)/shard_map/lij,ljk->lik/dot_general | solution.py:121
  1485.6 48.7 %fusion.47 = f32[4,768,768]{2,1,0:T(8,128)} fusion(f32[4,768,768]{2,1,0:T(8,128)S(1)} %copy-done.3, f32[4,768,768]{2,1,0:T(8,128)} %squeeze.42), kind=kOutput, calls=%fused_computation.83 | convolution fusion | flops 21743271936 | bytes 28311552 | tf_op jit(solution)/shard_map/lij,lik->ljk/dot_general | solution.py:122
  1534.4 13.7 stack.21
  1548.1 13.7 stack.22
  1561.7 9.6 maximum_bitcast_fusion
  1571.4 10.2 copy.36
  1585.9 24.8 fusion.23
  1610.7 519.3 %all-to-all-done.3 = f32[2,32,4,192,96]{4,3,2,0,1:T(8,128)} async-done(((f32[2,32,4,192,96]{4,3,2,0,1:T(8,128)}), f32[2,32,4,192,96]{4,3,2,0,1:T(8,128)}, u32[]{:S(2)}, u32[]{:S(2)}) %all-to-all-start.3) | async-done | bytes 18874400 | tf_op jit(solution)/shard_map/all_to_all | solution.py:86
  2130.0 17.9 copy.37
  2147.9 22.8 copy.38
  2170.7 10.8 multiply_dynamic-update-slice_fusion.4
  2185.9 11.3 multiply_dynamic-update-slice_fusion.3
  2197.2 11.8 multiply_dynamic-update-slice_fusion.2
  2209.1 11.3 multiply_dynamic-update-slice_fusion.1
  2220.4 18.4 multiply_dynamic-update-slice_fusion
  2238.9 46.0 %copy.40 = f32[640,18432]{1,0:T(8,128)} copy(f32[640,18432]{0,1:T(8,128)} %bitcast.163) | data formatting | bytes 94371840 | tf_op jit(solution)/shard_map/pc,pd->cd/dot_general | solution.py:136
  2284.9 49.1 %multiply_reduce_fusion.1 = (f32[128]{0:T(128)S(1)}, f32[192,96]{1,0:T(8,128)S(1)}, f32[192,96]{1,0:T(8,128)S(1)}, f32[192,96,128]{2,1,0:T(8,128)}) fusion(f32[192,96,128]{2,1,0:T(8,128)} %param.5, f32[192,96]{1,0:T(8,128)S(1)} %copy-done.9, f32[192,96]{1,0:T(8,128)S(1)} %copy-done.7, f32[128]{0:T(128)S(1)} %copy-done.14, ...), kind=kOutput, calls=%fused_computation.16 | convolution fusion | flops 18138230784 | bytes 66683904 | tf_op jit(solution)/shard_map/dot_general | solution.py:132
  2334.0 80.7 %fusion.48 = f32[128,5,128]{2,0,1:T(8,128)S(1)} fusion(f32[18432,128,1]{1,0,2:T(8,128)S(1)} %bitcast.166, f32[5,128,18432]{2,1,0:T(8,128)} %bitcast.162), kind=kOutput, calls=%fused_computation.84 | convolution fusion | flops 18119393280 | bytes 56950784 | tf_op jit(solution)/shard_map/pc,pd->cd/dot_general | solution.py:136
  2415.7 51.5 %all-reduce.3.cloned.1.call-done = f32[770,128]{1,0:T(8,128)} async-done(((f32[770,128]{1,0:T(8,128)}), f32[770,128]{1,0:T(8,128)}) %all-reduce.3.cloned.1.call-update) | async-done | bytes 394256 | tf_op jit(solution)/shard_map/psum | solution.py:147
  2467.2 13.8 subtract_multiply_fusion
  2480.9 35.2 %all-reduce.5.cloned.1.call-done = f32[770,128]{1,0:T(8,128)} async-done(((f32[770,128]{1,0:T(8,128)}), f32[770,128]{1,0:T(8,128)}) %all-reduce.5.cloned.1.call-update) | async-done | bytes 394256 | tf_op jit(solution)/shard_map/psum | solution.py:148
  (73 shorter events, 32.4 us)
Async XLA Ops:
  7.2 15.5 copy-start.16
  14.2 9.0 copy-start.6
  22.6 0.6 copy-start.8
  23.2 0.6 copy-start.13
  23.8 7.0 copy-start.10
  30.8 29.9 %copy-start.1 = (f32[192,96,128]{2,1,0:T(8,128)}, f32[192,96,128]{2,1,0:T(8,128)S(1)}, u32[]{:S(2)}) copy-start(f32[192,96,128]{2,1,0:T(8,128)S(1)} %fusion.10) | copy-start | bytes 28311556
  72.3 17.6 copy-start.4
  800.6 278.9 %all-to-all-start.1 = ((f32[1,32,4,192,96]{4,3,2,0,1:T(8,128)}), f32[1,32,4,192,96]{4,3,2,0,1:T(8,128)}, u32[]{:S(2)}, u32[]{:S(2)}) async-start(f32[1,32,4,192,96]{4,3,2,0,1:T(8,128)} %bitcast.175), calls=%async_computation.1 | async-start | bytes 25165824 | tf_op jit(solution)/shard_map/all_to_all | solution.py:75
  1091.2 7.2 copy-start
  1091.3 13.6 copy-start.12
  1458.3 27.3 %copy-start.3 = (f32[4,768,768]{2,1,0:T(8,128)S(1)}, f32[4,768,768]{2,1,0:T(8,128)}, u32[]{:S(2)}) copy-start(f32[4,768,768]{2,1,0:T(8,128)} %squeeze_reshape.3) | copy-start | bytes 28311556
  1581.6 548.4 %all-to-all-start.3 = ((f32[2,32,4,192,96]{4,3,2,0,1:T(8,128)}), f32[2,32,4,192,96]{4,3,2,0,1:T(8,128)}, u32[]{:S(2)}, u32[]{:S(2)}) async-start(f32[2,32,4,192,96]{4,3,2,0,1:T(8,128)} %bitcast.171), calls=%async_computation.3 | async-start | bytes 50331648 | tf_op jit(solution)/shard_map/all_to_all | solution.py:86
  1585.6 881.5 %all-reduce.3.cloned.1.call-start = ((), (), s32[]{:S(2)}) async-start(), calls=%async_computation.4 | async-start | bytes 794624 | tf_op jit(solution)/shard_map/psum | solution.py:147
  2147.9 22.8 copy-start.5
  2170.7 15.2 copy-start.2
  2197.2 23.2 slice-start
  2197.2 23.2 slice-start.1
  2209.1 11.3 slice-start.2
  2238.8 46.0 %copy-start.7 = (f32[192,96]{1,0:T(8,128)S(1)}, f32[192,96]{1,0:T(8,128)}, u32[]{:S(2)}) copy-start(f32[192,96]{1,0:T(8,128)} %copy-done.6) | copy-start | bytes 221188
  2238.8 46.0 %copy-start.9 = (f32[192,96]{1,0:T(8,128)S(1)}, f32[192,96]{1,0:T(8,128)}, u32[]{:S(2)}) copy-start(f32[192,96]{1,0:T(8,128)} %copy-done.8) | copy-start | bytes 221188
  2238.8 46.0 %copy-start.14 = (f32[128]{0:T(128)S(1)}, f32[128]{0:T(128)}, u32[]{:S(2)}) copy-start(f32[128]{0:T(128)} %copy-done.13) | copy-start | bytes 1540
  2284.8 49.1 %slice-start.3 = ((s8[9437184]{0:T(1024)(128)(4,1)}), s8[4194304]{0:T(1024)(128)(4,1)S(1)}, s32[]{:S(2)}) async-start(s8[9437184]{0:T(1024)(128)(4,1)} %bitcast.164), calls=%async_computation.9 | async-start | bytes 8388608
  2284.8 49.1 %slice-start.4 = ((s8[9437184]{0:T(1024)(128)(4,1)}), s8[4194304]{0:T(1024)(128)(4,1)S(1)}, s32[]{:S(2)}) async-start(s8[9437184]{0:T(1024)(128)(4,1)} %bitcast.164), calls=%async_computation.10 | async-start | bytes 8388608
  2284.9 49.1 %slice-start.5 = ((s8[9437184]{0:T(1024)(128)(4,1)}), s8[1048576]{0:T(1024)(128)(4,1)S(1)}, s32[]{:S(2)}) async-start(s8[9437184]{0:T(1024)(128)(4,1)} %bitcast.164), calls=%async_computation.11 | async-start | bytes 2097152
  2334.0 80.8 %copy-start.11 = (f32[128,128]{1,0:T(8,128)S(1)}, f32[128,128]{1,0:T(8,128)}, u32[]{:S(2)}) copy-start(f32[128,128]{1,0:T(8,128)} %fusion.23) | copy-start | bytes 196612
  2334.0 80.8 %copy-start.15 = (f32[128]{0:T(128)S(1)}, f32[128]{0:T(128)}, u32[]{:S(2)}) copy-start(f32[128]{0:T(128)} %get-tuple-element.5) | copy-start | bytes 1540
  2415.6 100.6 %all-reduce.5.cloned.1.call-start = ((), (), s32[]{:S(2)}) async-start(), calls=%async_computation.5 | async-start | bytes 794624 | tf_op jit(solution)/shard_map/psum | solution.py:148
Sparse Core Ops, SparseCore 0:
  2415.7 51.3 all-reduce.2
  2470.1 45.9 all-reduce.4
where the time goes:
time: 2530 us
  waiting for transfers between devices  869 us (34%)
  blocking collectives  830 us (33%)
  matrix products  347 us (14%)
  local copies, waits for them, and re-layouts  309 us (12%)
  other arithmetic  147 us (6%)
    all_to_all x1, blocking collectives, acts_to_channels(): lax.all_to_all(stacked, ('row', 'col'), split_axis=1, concat_axis=2, tile...  552 us
    all_to_all x1, waiting for transfers between devices, grads_to_positions(): lax.all_to_all(split_direct(chan_stack, tile_rows, tile_cols), ('row', 'c...  519 us
    all_to_all x1, blocking collectives, dtri_to_channels(): lax.all_to_all(stacked, ('row', 'col'), split_axis=1, concat_axis=2, tile...  279 us
    all_to_all x1, waiting for transfers between devices, tri_to_positions(): lax.all_to_all(split_direct(chan_stack, tile_rows, tile_cols), ('row', 'c...  263 us
    dot_general x7, matrix products, project(): return jnp.einsum('ijc,cd->ijd', operand, weight, precision=highest)  89.2 us
    dot_general x1, matrix products, on_device(): jnp.einsum('pc,pd->cd', flat_normed, grads_cat, precision=highest)  80.7 us
    psum x1, waiting for transfers between devices, on_device(): column_total = lax.psum(combined, 'col')  51.5 us
  transfers between devices with their start and end apart: 4, of which 4 were waited for; matrix products, arithmetic and copies ran while one was open for 2% of the time, Pallas kernels for 0%

commit v1 on v0

v1 whole, which is shorter than its diff:
```python
import jax
import jax.numpy as jnp
from jax import lax
from jax.sharding import PartitionSpec as P

epsilon = 1e-05
highest = lax.Precision.HIGH


def norm_parts(operand):
    average = jnp.mean(operand, axis=-1, keepdims=True)
    centered = operand - average
    inv_std = lax.rsqrt(jnp.mean(centered * centered, axis=-1, keepdims=True) + epsilon)
    return (centered * inv_std, inv_std)


def norm_back(grad_hat, normed, inv_std):
    first_mean = jnp.mean(grad_hat, axis=-1, keepdims=True)
    second_mean = jnp.mean(grad_hat * normed, axis=-1, keepdims=True)
    return inv_std * (grad_hat - first_mean - normed * second_mean)


def project(operand, weight):
    return jnp.einsum("ijc,cd->ijd", operand, weight, precision=highest)


def sigmoid(operand):
    return 1.0 / (1.0 + jnp.exp(-operand))


def chunk_count(channels):
    local_chans = channels // (lax.axis_size("row") * lax.axis_size("col"))
    return 2 if local_chans % 2 == 0 else 1


def exchange(blocks):
    return lax.all_to_all(blocks, ("row", "col"), split_axis=0, concat_axis=0, tiled=True)


def to_channels(tiles):
    tile_rows, tile_cols, channels = tiles.shape
    row_count = lax.axis_size("row")
    col_count = lax.axis_size("col")
    pieces = chunk_count(channels)
    blocks = jnp.transpose(tiles, (2, 0, 1)).reshape(
        row_count * col_count, pieces, -1, tile_rows, tile_cols
    )
    result = []
    for piece in range(pieces):
        arrived = exchange(blocks[:, piece])
        shaped = arrived.reshape(row_count, col_count, -1, tile_rows, tile_cols)
        shaped = jnp.transpose(shaped, (2, 0, 3, 1, 4))
        result.append(shaped.reshape(-1, row_count * tile_rows, col_count * tile_cols))
    return result


def send_back(chans, tile_rows, tile_cols):
    row_count = lax.axis_size("row")
    col_count = lax.axis_size("col")
    shaped = chans.reshape(-1, row_count, tile_rows, col_count, tile_cols)
    shaped = jnp.transpose(shaped, (1, 3, 0, 2, 4))
    return exchange(shaped.reshape(row_count * col_count, -1, tile_rows, tile_cols))


def to_positions(arrived):
    tile_rows, tile_cols = arrived[0].shape[2:]
    joined = jnp.stack(arrived, axis=1).reshape(-1, tile_rows, tile_cols)
    return jnp.transpose(joined, (1, 2, 0))


def on_device(pair_act, grad_out, residue_mask, norm_gains, weights):
    tile_rows, tile_cols, channels = pair_act.shape
    residues = residue_mask.shape[0]
    row_mask = lax.dynamic_slice_in_dim(residue_mask, lax.axis_index("row") * tile_rows, tile_rows)
    col_mask = lax.dynamic_slice_in_dim(residue_mask, lax.axis_index("col") * tile_cols, tile_cols)
    pair_mask = (row_mask[:, None] * col_mask[None, :]).astype(jnp.float32)[:, :, None]
    pair_hat, inv_std = norm_parts(pair_act)
    normed = pair_hat * norm_gains[0]
    lin_a = project(normed, weights[0])
    sig_a = sigmoid(project(normed, weights[1]))
    lin_b = project(normed, weights[2])
    sig_b = sigmoid(project(normed, weights[3]))
    chan_a = to_channels(pair_mask * sig_a * lin_a)
    chan_b = to_channels(pair_mask * sig_b * lin_b)
    tri_parts = []
    for left, right in zip(chan_a, chan_b):
        chan_tri = jnp.einsum("lik,ljk->lij", left, right, precision=highest)
        tri_parts.append(send_back(chan_tri, tile_rows, tile_cols))
    triangle = to_positions(tri_parts)
    tri_hat, tri_inv = norm_parts(triangle)
    tri_norm = tri_hat * norm_gains[1]
    lin_o = project(tri_norm, weights[5])
    sig_g = sigmoid(project(normed, weights[4]))
    d_out = grad_out * sig_g
    d_gate = grad_out * lin_o * sig_g * (1.0 - sig_g)
    d_norm = project(d_out, weights[5].T)
    d_tri = norm_back(d_norm * norm_gains[1], tri_hat, tri_inv)
    da_parts = []
    db_parts = []
    for left, right, chan_dtri in zip(chan_a, chan_b, to_channels(d_tri)):
        chan_da = jnp.einsum("lij,ljk->lik", chan_dtri, right, precision=highest)
        da_parts.append(send_back(chan_da, tile_rows, tile_cols))
        chan_db = jnp.einsum("lij,lik->ljk", chan_dtri, left, precision=highest)
        db_parts.append(send_back(chan_db, tile_rows, tile_cols))
    d_acts = [to_positions(da_parts), to_positions(db_parts)]
    d_lin_a = d_acts[0] * pair_mask * sig_a
    d_sig_a = d_acts[0] * pair_mask * lin_a * sig_a * (1.0 - sig_a)
    d_lin_b = d_acts[1] * pair_mask * sig_b
    d_sig_b = d_acts[1] * pair_mask * lin_b * sig_b * (1.0 - sig_b)
    grads_cat = jnp.concatenate([d_lin_a, d_sig_a, d_lin_b, d_sig_b, d_gate], axis=-1).reshape(
        -1, 5 * channels
    )
    weights_turned = jnp.transpose(weights[:5], (0, 2, 1)).reshape(5 * channels, channels)
    d_normed = jnp.dot(grads_cat, weights_turned, precision=highest).reshape(
        tile_rows, tile_cols, channels
    )
    flat_normed = normed.reshape(-1, channels)
    weight_part = jnp.einsum("pc,pd->cd", flat_normed, grads_cat, precision=highest)
    weight_part = jnp.transpose(weight_part.reshape(channels, 5, channels), (1, 0, 2)).reshape(
        5 * channels, channels
    )
    out_part = jnp.einsum(
        "pc,pd->cd", tri_norm.reshape(-1, channels), d_out.reshape(-1, channels), precision=highest
    )
    gain_one = jnp.sum(d_normed * pair_hat, axis=(0, 1))
    gain_two = jnp.sum(d_norm * tri_hat, axis=(0, 1))
    grad_pair = norm_back(d_normed * norm_gains[0], pair_hat, inv_std)
    combined = jnp.concatenate([weight_part, out_part, gain_one[None], gain_two[None]], axis=0)
    column_total = lax.psum(combined, "col")
    total = lax.psum(column_total, "row")
    scaled = total / residues
    grad_weights = scaled[: 6 * channels].reshape(6, channels, channels)
    grad_gains = scaled[6 * channels :]
    return (grad_pair, grad_weights, grad_gains)


def solution(mesh):
    return jax.shard_map(
        on_device,
        mesh=mesh,
        in_specs=(P("row", "col", None), P("row", "col", None), P(), P(), P()),
        out_specs=(P("row", "col", None), P(), P()),
        check_vma=False,
    )
```

time: 2530 us -> 2250 us (0.89)
  blocking collectives: 830 us -> 429 us
  waiting for transfers between devices: 869 us -> 1020 us
  matrix products: 347 us -> 221 us
  local copies, waits for them, and re-layouts: 309 us -> 347 us
  starting transfers between devices: 8.4 us -> 37.3 us
    all_to_all x2 -> x3, blocking collectives: 830 us -> 429 us  [exchange(): lax.all_to_all(blocks, ('row', 'col'), split_axis=0, concat_axis=0, tiled...]
    all_to_all x2 -> x9, waiting for transfers between devices: 782 us -> 938 us  [exchange(): lax.all_to_all(blocks, ('row', 'col'), split_axis=0, concat_axis=0, tiled...]
    reshape x4 -> x23, local copies, waits for them, and re-layouts: 81.6 us -> 193 us  [the longest x8 59.9 us: send_back(): shaped = chans.reshape(-1, row_count, tile_rows, col_count, tile_cols)]
    another operation x5 -> x1, local copies, waits for them, and re-layouts: 65.8 us -> 10.7 us  [to_positions(): joined = jnp.stack(arrived, axis=1).reshape(-1, tile_rows, tile_cols)]
    dot_general x3 -> x6, matrix products: 104 us -> 64.5 us  [the longest x2 21.7 us: on_device(): chan_db = jnp.einsum('lij,lik->ljk', chan_dtri, left, precision=highest)]
    dot_general x1, matrix products: 80.7 us -> 44 us  [on_device(): jnp.einsum('pc,pd->cd', flat_normed, grads_cat, precision=highest)]
    mul x0 -> x3, local copies, waits for them, and re-layouts: none -> 35.1 us  [the longest x1 11.9 us: on_device(): chan_a = to_channels(pair_mask * sig_a * lin_a)]
    transpose x3 -> x0, other arithmetic: 32.7 us -> none  [the longest x2 23.1 us: channel_major(): return jnp.transpose(tiles, (0, 3, 1, 2))]
  transfers between devices with their start and end apart: 4 -> 11, of which waited for: 4 -> 11; matrix products, arithmetic and copies ran while one was open for 2% -> 15% of each run, Pallas kernels for 0% -> 0%
where the time goes in v1:
time: 2250 us; the launch traced here: 2240 us
  waiting for transfers between devices  1020 us (45%)
  blocking collectives  429 us (19%)
  local copies, waits for them, and re-layouts  347 us (15%)
  matrix products  221 us (10%)
  other arithmetic  171 us (8%)
  starting transfers between devices  37.3 us (2%)
    all_to_all x9, waiting for transfers between devices, exchange(): lax.all_to_all(blocks, ('row', 'col'), split_axis=0, concat_axis=0, tiled...  938 us
    all_to_all x3, blocking collectives, exchange(): lax.all_to_all(blocks, ('row', 'col'), split_axis=0, concat_axis=0, tiled...  429 us
    dot_general x7, matrix products, project(): return jnp.einsum('ijc,cd->ijd', operand, weight, precision=highest)  63.6 us
    reshape x8, local copies, waits for them, and re-layouts, send_back(): shaped = chans.reshape(-1, row_count, tile_rows, col_count, tile_cols)  59.9 us
    reshape x6, local copies, waits for them, and re-layouts, to_channels(): shaped = arrived.reshape(row_count, col_count, -1, tile_rows, tile_cols)  53.9 us
    unnamed x8, other arithmetic  51.9 us
    psum x1, waiting for transfers between devices, on_device(): column_total = lax.psum(combined, 'col')  51.5 us
    dot_general x1, local copies, waits for them, and re-layouts, on_device(): jnp.einsum('pc,pd->cd', flat_normed, grads_cat, precision=highest)  45.9 us
  transfers between devices with their start and end apart: 11, of which 11 were waited for; matrix products, arithmetic and copies ran while one was open for 15% of the time, Pallas kernels for 0%

profile of v1, /device:TPU:0, one launch (start us, length us, event | category | flops | bytes accessed | tf_op | source)
XLA Modules:
  0.0 2244.1 jit_solution(10932491899332738724)
XLA Ops:
  57.7 21.0 multiply_bitcast_fusion
  78.7 11.9 copy.23
  90.6 10.8 slice_bitcast_fusion.5
  108.8 11.6 copy.25
  120.4 10.8 slice_bitcast_fusion.4
  131.2 117.4 %all-to-all-done = f32[32,2,192,96]{3,2,1,0:T(8,128)} async-done(((f32[32,2,192,96]{3,2,1,0:T(8,128)}), f32[32,2,192,96]{3,2,1,0:T(8,128)}, u32[]{:S(2)}, u32[]{:S(2)}) %all-to-all-start) | async-done | bytes 4718624 | tf_op jit(solution)/shard_map/all_to_all | solution.py:37
  248.7 144.0 %all_to_all.60 = f32[32,2,192,96]{3,2,1,0:T(8,128)} all-to-all(f32[32,2,192,96]{3,2,1,0:T(8,128)} %get-tuple-element.11), channel_id=1, replica_groups=mesh['row'=4,'col'=8] {'row','col'}, dimensions={0} | all-to-all | bytes 9437184 | tf_op jit(solution)/shard_map/all_to_all | solution.py:37
  392.6 142.3 %all_to_all.61 = f32[32,2,192,96]{3,2,1,0:T(8,128)} all-to-all(f32[32,2,192,96]{3,2,1,0:T(8,128)S(1)} %bitcast.223), channel_id=1, replica_groups=mesh['row'=4,'col'=8] {'row','col'}, dimensions={0} | all-to-all | bytes 9437184 | tf_op jit(solution)/shard_map/all_to_all | solution.py:37
  538.5 9.0 copy.63
  571.2 10.5 fusion.49
  596.1 82.2 %all-to-all-done.4 = f32[32,2,192,96]{3,2,1,0:T(8,128)} async-done(((f32[32,2,192,96]{3,2,1,0:T(8,128)}), f32[32,2,192,96]{3,2,1,0:T(8,128)}, u32[]{:S(2)}, u32[]{:S(2)}) %all-to-all-start.4) | async-done | bytes 4718624 | tf_op jit(solution)/shard_map/all_to_all | solution.py:37
  682.0 9.0 copy.61
  698.5 9.0 copy.60
  714.9 10.6 fusion.50
  740.2 81.7 %all-to-all-done.2 = f32[32,2,192,96]{3,2,1,0:T(8,128)} async-done(((f32[32,2,192,96]{3,2,1,0:T(8,128)}), f32[32,2,192,96]{3,2,1,0:T(8,128)}, u32[]{:S(2)}, u32[]{:S(2)}) %all-to-all-start.2) | async-done | bytes 4718624 | tf_op jit(solution)/shard_map/all_to_all | solution.py:37
  834.1 131.3 %all-to-all-done.5 = f32[32,2,192,96]{3,2,1,0:T(8,128)} async-done(((f32[32,2,192,96]{3,2,1,0:T(8,128)}), f32[32,2,192,96]{3,2,1,0:T(8,128)}, u32[]{:S(2)}, u32[]{:S(2)}) %all-to-all-start.5) | async-done | bytes 4718624 | tf_op jit(solution)/shard_map/all_to_all | solution.py:37
  965.3 11.6 pad_maximum_fusion
  977.0 10.7 copy.31
  987.7 11.7 copy.32
  1013.0 16.4 multiply_reduce_fusion
  1029.4 12.2 fusion.8
  1041.6 11.6 copy.34
  1061.8 142.3 %all_to_all.62 = f32[32,2,192,96]{3,2,1,0:T(8,128)} all-to-all(f32[32,2,192,96]{3,2,1,0:T(8,128)S(1)} %get-tuple-element.9), channel_id=1, replica_groups=mesh['row'=4,'col'=8] {'row','col'}, dimensions={0} | all-to-all | bytes 9437184 | tf_op jit(solution)/shard_map/all_to_all | solution.py:37
  1224.2 10.9 fusion.53
  1249.4 98.3 %all-to-all-done.8 = f32[32,2,192,96]{3,2,1,0:T(8,128)} async-done(((f32[32,2,192,96]{3,2,1,0:T(8,128)}), f32[32,2,192,96]{3,2,1,0:T(8,128)}, u32[]{:S(2)}, u32[]{:S(2)}) %all-to-all-start.8) | async-done | bytes 4718624 | tf_op jit(solution)/shard_map/all_to_all | solution.py:37
  1367.9 10.8 fusion.54
  1393.0 98.4 %all-to-all-done.10 = f32[32,2,192,96]{3,2,1,0:T(8,128)} async-done(((f32[32,2,192,96]{3,2,1,0:T(8,128)}), f32[32,2,192,96]{3,2,1,0:T(8,128)}, u32[]{:S(2)}, u32[]{:S(2)}) %all-to-all-start.10) | async-done | bytes 4718624 | tf_op jit(solution)/shard_map/all_to_all | solution.py:37
  1495.5 10.9 fusion.51
  1520.6 114.7 %all-to-all-done.11 = f32[32,2,192,96]{3,2,1,0:T(8,128)} async-done(((f32[32,2,192,96]{3,2,1,0:T(8,128)}), f32[32,2,192,96]{3,2,1,0:T(8,128)}, u32[]{:S(2)}, u32[]{:S(2)}) %all-to-all-start.11) | async-done | bytes 4718624 | tf_op jit(solution)/shard_map/all_to_all | solution.py:37
  1639.0 10.8 fusion.52
  1664.1 114.8 %all-to-all-done.7 = f32[32,2,192,96]{3,2,1,0:T(8,128)} async-done(((f32[32,2,192,96]{3,2,1,0:T(8,128)}), f32[32,2,192,96]{3,2,1,0:T(8,128)}, u32[]{:S(2)}, u32[]{:S(2)}) %all-to-all-start.7) | async-done | bytes 4718624 | tf_op jit(solution)/shard_map/all_to_all | solution.py:37
  1783.5 16.6 fusion.28
  1800.1 11.6 pad_maximum_fusion.2
  1811.7 11.7 copy.44
  1823.4 98.9 %all-to-all-done.9 = f32[32,2,192,96]{3,2,1,0:T(8,128)} async-done(((f32[32,2,192,96]{3,2,1,0:T(8,128)}), f32[32,2,192,96]{3,2,1,0:T(8,128)}, u32[]{:S(2)}, u32[]{:S(2)}) %all-to-all-start.9) | async-done | bytes 4718624 | tf_op jit(solution)/shard_map/all_to_all | solution.py:37
  1922.3 11.6 pad_maximum_fusion.1
  1933.9 11.7 copy.39
  1945.6 12.0 fusion.4
  1957.7 11.2 fusion.7
  1968.9 12.7 fusion
  1981.6 16.0 fusion.3
  1998.2 13.1 multiply_dynamic-update-slice_fusion
  2011.4 45.9 %copy.46 = f32[640,18432]{1,0:T(8,128)} copy(f32[640,18432]{0,1:T(8,128)} %bitcast.200) | data formatting | bytes 94371840 | tf_op jit(solution)/shard_map/pc,pd->cd/dot_general | solution.py:118
  2057.3 32.0 %multiply_reduce_fusion.1 = (f32[128]{0:T(128)S(1)}, f32[192,96]{1,0:T(8,128)S(1)}, f32[192,96]{1,0:T(8,128)S(1)}, f32[192,96,128]{2,1,0:T(8,128)}) fusion(f32[192,96,128]{2,1,0:T(8,128)} %param.5, f32[192,96]{1,0:T(8,128)S(1)} %copy-done.8, f32[192,96]{1,0:T(8,128)S(1)} %copy-done.6, f32[128]{0:T(128)S(1)} %copy-done.13, ...), kind=kOutput, calls=%fused_computation.22 | convolution fusion | flops 9078534144 | bytes 66683904 | tf_op jit(solution)/shard_map/dot_general | solution.py:114
  2089.3 44.0 %fusion.55 = f32[128,5,128]{2,0,1:T(8,128)S(1)} fusion(f32[18432,128,1]{1,0,2:T(8,128)} %bitcast.202, f32[5,128,18432]{2,1,0:T(8,128)} %bitcast.201), kind=kOutput, calls=%fused_computation.99 | convolution fusion | flops 9059696640 | bytes 56950784 | tf_op jit(solution)/shard_map/pc,pd->cd/dot_general | solution.py:118
  2134.2 51.5 %all-reduce.3.cloned.1.call-done = f32[770,128]{1,0:T(8,128)} async-done(((f32[770,128]{1,0:T(8,128)}), f32[770,128]{1,0:T(8,128)}) %all-reduce.3.cloned.1.call-update) | async-done | bytes 394256 | tf_op jit(solution)/shard_map/psum | solution.py:129
  2185.6 13.8 subtract_multiply_fusion
  2199.4 35.2 %all-reduce.5.cloned.1.call-done = f32[770,128]{1,0:T(8,128)} async-done(((f32[770,128]{1,0:T(8,128)}), f32[770,128]{1,0:T(8,128)}) %all-reduce.5.cloned.1.call-update) | async-done | bytes 394256 | tf_op jit(solution)/shard_map/psum | solution.py:130
  (122 shorter events, 280.4 us)
Async XLA Ops:
  7.2 15.2 copy-start.16
  14.2 8.7 copy-start.5
  22.4 0.6 copy-start.7
  22.9 0.6 copy-start.12
  23.5 7.0 copy-start.10
  30.5 19.4 copy-start.1
  57.7 21.0 copy-start.3
  101.4 147.3 %all-to-all-start = ((f32[32,2,192,96]{3,2,1,0:T(8,128)}), f32[32,2,192,96]{3,2,1,0:T(8,128)}, u32[]{:S(2)}, u32[]{:S(2)}) async-start(f32[32,2,192,96]{3,2,1,0:T(8,128)} %get-tuple-element.13), calls=%async_computation | async-start | bytes 12582912 | tf_op jit(solution)/shard_map/all_to_all | solution.py:37
  131.2 261.4 %slice-start.9 = ((s8[6291456]{0:T(1024)(128)(4,1)}), s8[2097152]{0:T(1024)(128)(4,1)S(1)}, s32[]{:S(2)}) async-start(s8[6291456]{0:T(1024)(128)(4,1)} %bitcast.222), calls=%async_computation.23 | async-start | bytes 4194304
  248.6 144.0 %slice-start.10 = ((s8[6291456]{0:T(1024)(128)(4,1)}), s8[4194304]{0:T(1024)(128)(4,1)S(1)}, s32[]{:S(2)}) async-start(s8[6291456]{0:T(1024)(128)(4,1)} %bitcast.222), calls=%async_computation.24 | async-start | bytes 8388608
  534.9 143.5 %all-to-all-start.4 = ((f32[32,2,192,96]{3,2,1,0:T(8,128)}), f32[32,2,192,96]{3,2,1,0:T(8,128)}, u32[]{:S(2)}, u32[]{:S(2)}) async-start(f32[32,2,192,96]{3,2,1,0:T(8,128)} %get-tuple-element.12), calls=%async_computation.4 | async-start | bytes 12582912 | tf_op jit(solution)/shard_map/all_to_all | solution.py:37
  678.4 143.5 %all-to-all-start.2 = ((f32[32,2,192,96]{3,2,1,0:T(8,128)}), f32[32,2,192,96]{3,2,1,0:T(8,128)}, u32[]{:S(2)}, u32[]{:S(2)}) async-start(f32[32,2,192,96]{3,2,1,0:T(8,128)} %bitcast.214), calls=%async_computation.2 | async-start | bytes 12582912 | tf_op jit(solution)/shard_map/all_to_all | solution.py:37
  821.9 143.5 %all-to-all-start.5 = ((f32[32,2,192,96]{3,2,1,0:T(8,128)}), f32[32,2,192,96]{3,2,1,0:T(8,128)}, u32[]{:S(2)}, u32[]{:S(2)}) async-start(f32[32,2,192,96]{3,2,1,0:T(8,128)} %bitcast.220), calls=%async_computation.5 | async-start | bytes 12582912 | tf_op jit(solution)/shard_map/all_to_all | solution.py:37
  999.4 7.2 copy-start
  999.4 13.6 copy-start.14
  1204.1 143.6 %all-to-all-start.8 = ((f32[32,2,192,96]{3,2,1,0:T(8,128)}), f32[32,2,192,96]{3,2,1,0:T(8,128)}, u32[]{:S(2)}, u32[]{:S(2)}) async-start(f32[32,2,192,96]{3,2,1,0:T(8,128)} %get-tuple-element.10), calls=%async_computation.8 | async-start | bytes 12582912 | tf_op jit(solution)/shard_map/all_to_all | solution.py:37
  1347.7 143.7 %all-to-all-start.10 = ((f32[32,2,192,96]{3,2,1,0:T(8,128)}), f32[32,2,192,96]{3,2,1,0:T(8,128)}, u32[]{:S(2)}, u32[]{:S(2)}) async-start(f32[32,2,192,96]{3,2,1,0:T(8,128)} %bitcast.216), calls=%async_computation.10 | async-start | bytes 12582912 | tf_op jit(solution)/shard_map/all_to_all | solution.py:37
  1491.4 143.9 %all-to-all-start.11 = ((f32[32,2,192,96]{3,2,1,0:T(8,128)}), f32[32,2,192,96]{3,2,1,0:T(8,128)}, u32[]{:S(2)}, u32[]{:S(2)}) async-start(f32[32,2,192,96]{3,2,1,0:T(8,128)} %bitcast.217), calls=%async_computation.11 | async-start | bytes 12582912 | tf_op jit(solution)/shard_map/all_to_all | solution.py:37
  1635.4 143.5 %all-to-all-start.7 = ((f32[32,2,192,96]{3,2,1,0:T(8,128)}), f32[32,2,192,96]{3,2,1,0:T(8,128)}, u32[]{:S(2)}, u32[]{:S(2)}) async-start(f32[32,2,192,96]{3,2,1,0:T(8,128)} %bitcast.218), calls=%async_computation.7 | async-start | bytes 12582912 | tf_op jit(solution)/shard_map/all_to_all | solution.py:37
  1664.1 118.5 %copy-start.11 = (f32[6,128,128]{2,1,0:T(8,128)S(1)}, f32[6,128,128]{2,1,0:T(8,128)}, u32[]{:S(2)}) copy-start(f32[6,128,128]{2,1,0:T(8,128)} %param.9) | copy-start | bytes 1179652
  1778.9 143.5 %all-to-all-start.9 = ((f32[32,2,192,96]{3,2,1,0:T(8,128)}), f32[32,2,192,96]{3,2,1,0:T(8,128)}, u32[]{:S(2)}, u32[]{:S(2)}) async-start(f32[32,2,192,96]{3,2,1,0:T(8,128)} %bitcast.215), calls=%async_computation.9 | async-start | bytes 12582912 | tf_op jit(solution)/shard_map/all_to_all | solution.py:37
  1782.5 403.2 %all-reduce.3.cloned.1.call-start = ((), (), s32[]{:S(2)}) async-start(), calls=%async_computation.12 | async-start | bytes 794624 | tf_op jit(solution)/shard_map/psum | solution.py:129
  1933.9 11.7 copy-start.4
  1945.6 12.0 copy-start.2
  1968.9 28.7 %slice-start = ((s8[9437184]{0:T(1024)(128)(4,1)}), s8[4194304]{0:T(1024)(128)(4,1)S(1)}, s32[]{:S(2)}) async-start(s8[9437184]{0:T(1024)(128)(4,1)} %bitcast.198), calls=%async_computation.14 | async-start | bytes 8388608
  1968.9 28.7 %slice-start.1 = ((s8[9437184]{0:T(1024)(128)(4,1)}), s8[4194304]{0:T(1024)(128)(4,1)S(1)}, s32[]{:S(2)}) async-start(s8[9437184]{0:T(1024)(128)(4,1)} %bitcast.198), calls=%async_computation.15 | async-start | bytes 8388608
  1968.9 28.7 %slice-start.3 = ((s8[9437184]{0:T(1024)(128)(4,1)}), s8[4194304]{0:T(1024)(128)(4,1)S(1)}, s32[]{:S(2)}) async-start(s8[9437184]{0:T(1024)(128)(4,1)} %bitcast.203), calls=%async_computation.17 | async-start | bytes 8388608
  1968.9 28.7 %slice-start.4 = ((s8[9437184]{0:T(1024)(128)(4,1)}), s8[4194304]{0:T(1024)(128)(4,1)S(1)}, s32[]{:S(2)}) async-start(s8[9437184]{0:T(1024)(128)(4,1)} %bitcast.203), calls=%async_computation.18 | async-start | bytes 8388608
  1968.9 28.7 %slice-start.6 = ((s8[9437184]{0:T(1024)(128)(4,1)}), s8[4194304]{0:T(1024)(128)(4,1)S(1)}, s32[]{:S(2)}) async-start(s8[9437184]{0:T(1024)(128)(4,1)} %bitcast.205), calls=%async_computation.20 | async-start | bytes 8388608
  1968.9 28.7 %slice-start.7 = ((s8[9437184]{0:T(1024)(128)(4,1)}), s8[4194304]{0:T(1024)(128)(4,1)S(1)}, s32[]{:S(2)}) async-start(s8[9437184]{0:T(1024)(128)(4,1)} %bitcast.205), calls=%async_computation.21 | async-start | bytes 8388608
  1981.6 16.1 slice-start.2
  1981.6 16.1 slice-start.5
  1981.6 16.6 slice-start.8
  2011.3 45.9 %copy-start.6 = (f32[192,96]{1,0:T(8,128)S(1)}, f32[192,96]{1,0:T(8,128)}, u32[]{:S(2)}) copy-start(f32[192,96]{1,0:T(8,128)} %copy-done.5) | copy-start | bytes 221188
  2011.3 45.9 %copy-start.8 = (f32[192,96]{1,0:T(8,128)S(1)}, f32[192,96]{1,0:T(8,128)}, u32[]{:S(2)}) copy-start(f32[192,96]{1,0:T(8,128)} %copy-done.7) | copy-start | bytes 221188
  2011.3 45.9 %copy-start.9 = (f32[5,128,128]{2,1,0:T(8,128)S(1)}, f32[5,128,128]{2,1,0:T(8,128)}, u32[]{:S(2)}) copy-start(f32[5,128,128]{2,1,0:T(8,128)} %copy.45) | copy-start | bytes 983044
  2011.3 45.9 %copy-start.13 = (f32[128]{0:T(128)S(1)}, f32[128]{0:T(128)}, u32[]{:S(2)}) copy-start(f32[128]{0:T(128)} %copy-done.12) | copy-start | bytes 1540
  2089.3 44.0 %copy-start.15 = (f32[128]{0:T(128)S(1)}, f32[128]{0:T(128)}, u32[]{:S(2)}) copy-start(f32[128]{0:T(128)} %get-tuple-element.5) | copy-start | bytes 1540
  2134.1 100.5 %all-reduce.5.cloned.1.call-start = ((), (), s32[]{:S(2)}) async-start(), calls=%async_computation.13 | async-start | bytes 794624 | tf_op jit(solution)/shard_map/psum | solution.py:130
Sparse Core Ops, SparseCore 0:
  2134.2 51.3 all-reduce.2
  2188.6 45.9 all-reduce.4
